TPU v7x, 32 devices: a whole 2x2x4 slice. The times are simulated.
32 devices in a mesh: groups: 2 (over x), blk: 16 (over z, y, core).
Axes of the slice: x: 2, y: 2, z: 4, core: 2. Of those that a mesh axis runs over, the one named last changes fastest.
Arguments:
- embeddings: bfloat16 [12288, 512], P(('groups', 'blk')), parts along dimension 0, may hold values from -24 to 24
- cluster_ids: int32 [12288], P(('groups', 'blk')), parts along dimension 0, may hold values from 0 to 63, as said below
- cluster_sizes: int32 [128], P('groups'), parts along dimension 0, may hold values from 12 to 960, as said below
Outputs:
- log_density: float32 [12288], P(('groups', 'blk')), parts along dimension 0
- centrality: float32 [12288], P(('groups', 'blk')), parts along dimension 0
There are 2 independent parts, one for each index of `groups`. A program takes and returns all parts, laid end to end along the dimension named above; each array names one. Nothing has to cross between parts.
Inputs may be any that keep to these rules, and one draw needn't show every extreme that they name: cluster_sizes[c] is the number of rows whose cluster id is c; the sizes sum to 6144 and the largest is exactly 960. `cluster_ids`: rows are dealt to the devices of blk: with n the number of devices of blk and E_c the sum of cluster_sizes[c'] mod n over the clusters c' < c, device s holds cluster_sizes[c] // n rows of cluster c, plus one more exactly when (s - E_c) mod n < cluster_sizes[c] mod n. Within a device the rows stand in no particular order.
All inputs are finite; a program needn't handle non-finite values.
Results may differ from a plain program's by a relative error of at most 0.00065.
The roundings to bfloat16 on the way count: a program that leaves them out, or rounds other values in their place, can miss the bound.
Values may be sent and summed in bfloat16 or wider, within the bound.
No kernel may reach another device: no remote copies, remote signals or barrier semaphores. Data moves between devices by JAX's collectives and lax.ppermute only.
A program may use at most 64 MiB of HBM per device.

v0:
```python
import jax
import jax.numpy as jnp
from jax import lax
from jax.sharding import PartitionSpec as P

SOFTMAX_TEMP = 0.1
EPSILON = 1e-06


def shifted(array, axis, by):
    peers = lax.axis_size(axis)
    pairs = [(i, i + by) for i in range(peers) if 0 <= i + by < peers]
    return lax.ppermute(array, axis, pairs)


def unit_rows(embeddings):
    values = embeddings.astype(jnp.float32)
    scale = lax.rsqrt(jnp.mean(values * values, axis=1, keepdims=True) + EPSILON)
    return (values * (scale * values.shape[1] ** (-0.5))).astype(jnp.bfloat16)


def block_terms(remaining_rows, left_labels, right_rows, right_labels):
    similarity_scores = jnp.einsum(
        "rd,kd->rk", remaining_rows, right_rows, preferred_element_type=jnp.float32
    )
    same_cluster = left_labels[:, None] == right_labels[None, :]
    return jnp.sum(jnp.where(same_cluster, jnp.exp(similarity_scores / SOFTMAX_TEMP), 0.0), axis=1)


def lookup(table, one_hot):
    return jnp.sum(jnp.where(one_hot, table[None, :], 0), axis=1)


def sorted_density(unit, cluster_sizes, member):
    devices = lax.axis_size("blk")
    own_index = lax.axis_index("blk")
    rows_dev = unit.shape[0]
    clusters = cluster_sizes.shape[0]
    total_rows = rows_dev * devices
    fewest = total_rows // 512
    largest = total_rows * 5 // 32
    capacity = min(rows_dev, rows_dev // devices + rows_dev // fewest + 2)
    reach = (largest + rows_dev - 2) // rows_dev
    ends = jnp.cumsum(cluster_sizes)
    starts = ends - cluster_sizes
    base = cluster_sizes // devices
    extra = cluster_sizes % devices
    first = (jnp.cumsum(extra) - extra) % devices
    source_rows = jnp.arange(devices, dtype=jnp.int32)
    holds = base[None, :] + (
        (source_rows[:, None] - first[None, :]) % devices < extra[None, :]
    ).astype(jnp.int32)
    member_count = jnp.cumsum(member.astype(jnp.int32), axis=0)
    rank = jnp.sum(jnp.where(member, member_count - 1, 0), axis=1)
    held_row = jnp.dot(
        member.astype(jnp.float32), holds.T.astype(jnp.float32), precision=lax.Precision.HIGHEST
    ).astype(jnp.int32)
    before_me = (source_rows[None, :] < own_index) & (held_row > rank[:, None])
    within = jnp.sum(jnp.minimum(held_row, rank[:, None]), axis=1) + jnp.sum(
        before_me.astype(jnp.int32), axis=1
    )
    position = lookup(starts, member) + within
    target = position // rows_dev
    earlier = (target[None, :] == target[:, None]) & (position[None, :] < position[:, None])
    slot = jnp.sum(earlier.astype(jnp.int32), axis=1)
    address = target * capacity + slot
    sender = (
        jnp.zeros((devices * capacity,), jnp.int32)
        .at[address]
        .set(jnp.arange(rows_dev, dtype=jnp.int32))
    )
    filled = jnp.zeros((devices * capacity,), jnp.bool_).at[address].set(True)
    packed = jnp.where(filled[:, None], unit[sender], jnp.zeros((), jnp.bfloat16))
    arrived = lax.all_to_all(packed, "blk", split_axis=0, concat_axis=0, tiled=True)
    local = jnp.arange(rows_dev, dtype=jnp.int32)
    places = own_index * rows_dev + local
    home_label = jnp.sum((places[:, None] >= ends[None, :]).astype(jnp.int32), axis=1)
    home_cluster_member = home_label[:, None] == jnp.arange(clusters, dtype=jnp.int32)[None, :]
    offset_in = places - lookup(starts, home_cluster_member)
    base_row = lookup(base, home_cluster_member)
    extra_row = lookup(extra, home_cluster_member)
    first_row = lookup(first, home_cluster_member)
    full_rounds = devices * base_row
    surplus = offset_in - full_rounds
    wrapped = first_row + extra_row - devices
    late_source = jnp.where(
        wrapped > 0,
        jnp.where(surplus < wrapped, surplus, first_row + surplus - wrapped),
        first_row + surplus,
    )
    anchor = jnp.where(offset_in < full_rounds, offset_in % devices, late_source)
    anchor_hot = anchor[:, None] == source_rows[None, :]
    anchor_count = jnp.cumsum(anchor_hot.astype(jnp.int32), axis=0)
    order_in = jnp.sum(jnp.where(anchor_hot, anchor_count - 1, 0), axis=1)
    block = arrived[anchor * capacity + order_in]

    def labels_at(spots):
        inside = (spots >= 0) & (spots < total_rows)
        found = jnp.sum((spots[:, None] >= ends[None, :]).astype(jnp.int32), axis=1)
        return jnp.where(inside, found, -1)

    density = block_terms(block, home_label, block, home_label)

    def advance(offset, carried_rows):
        upper, lower, running = carried_rows
        upper = shifted(upper, "blk", 1)
        lower = shifted(lower, "blk", -1)
        running = running + block_terms(
            block, home_label, upper, labels_at(places - offset * rows_dev)
        )
        running = running + block_terms(
            block, home_label, lower, labels_at(places + offset * rows_dev)
        )
        return (upper, lower, running)

    carried_out = lax.fori_loop(1, reach + 1, advance, (block, block, density))
    density = carried_out[2]
    returned = (
        jnp.zeros((devices * capacity,), jnp.float32).at[anchor * capacity + order_in].set(density)
    )
    answered = lax.all_to_all(returned, "blk", split_axis=0, concat_axis=0, tiled=True)
    return answered[address]


def on_device(embeddings, cluster_ids, cluster_sizes):
    unit = unit_rows(embeddings)
    clusters = cluster_sizes.shape[0]
    member = cluster_ids[:, None] == jnp.arange(clusters, dtype=jnp.int32)[None, :]
    partial_sum = jnp.einsum(
        "rc,rd->cd", member.astype(jnp.bfloat16), unit, preferred_element_type=jnp.float32
    )
    centroid = lax.psum(partial_sum, "blk")
    density = sorted_density(unit, cluster_sizes, member)
    sizes_row = lookup(cluster_sizes, member).astype(jnp.float32)
    log_density = jnp.log(density / sizes_row)
    projected = jnp.dot(unit.astype(jnp.float32), centroid.T, precision=lax.Precision.HIGHEST)
    centrality = jnp.sum(jnp.where(member, projected, 0.0), axis=1) / sizes_row
    return (log_density, centrality)


def solution(mesh):
    in_specs = (P(("groups", "blk"), None), P(("groups", "blk")), P("groups"))
    out_specs = (P(("groups", "blk")), P(("groups", "blk")))
    return jax.shard_map(
        on_device, mesh=mesh, in_specs=in_specs, out_specs=out_specs, check_vma=False
    )
```

profile of v0, /device:TPU:8, one launch (start us, length us, event | category | flops | bytes accessed | tf_op | source)
XLA Modules:
  0.0 142.4 jit_solution(12733876175211087510)
XLA Ops:
  7.2 1.2 fusion.14
  8.6 0.6 copy-done.2
  10.0 0.6 copy-done.1
  10.6 0.9 reduce-window.41
  12.6 2.9 %scatter_custom_fusion.1 = s32[928]{0:T(1024)S(1)} fusion(s32[384]{0:T(512)S(1)} %fusion.58, s32[384]{0:T(512)S(1)} %iota.57, s32[]{:T(128)} %copy.40), kind=kCustom, calls=%fused_computation.120 | custom fusion | bytes 3716 | tf_op jit(solution)/shard_map/scatter | solution.py:70
  15.5 4.0 %gather_fusion = bf16[928,512]{1,0:T(8,128)(2,1)S(1)} fusion(bf16[384,512]{1,0:T(8,128)(2,1)S(1)} %fusion.15, s32[1024]{0:T(1024)S(1)} %pad_clamp_fusion.2), kind=kCustom, calls=%fused_computation | custom fusion | bytes 1904256 | tf_op jit(solution)/shard_map/gather | solution.py:73
  19.8 2.0 %scatter_custom_fusion = pred[928]{0:T(1024)(128)(4,1)S(1)} fusion(s32[384]{0:T(512)S(1)} %fusion.58, pred[384]{0:T(512)(128)(4,1)S(1)} %broadcast.470, pred[]{:T(512)} %constant.152.clone.1), kind=kCustom, calls=%fused_computation.132 | custom fusion | bytes 929 | tf_op jit(solution)/shard_map/scatter | solution.py:72
  21.9 1.2 broadcast_select_fusion
  23.1 6.3 %all-to-all-start = ((bf16[16,58,512]{2,1,0:T(8,128)(2,1)}), bf16[16,58,512]{2,1,0:T(8,128)(2,1)S(1)}, u32[]{:S(2)}, u32[]{:S(2)}) async-start(bf16[16,58,512]{2,1,0:T(8,128)(2,1)} %broadcast_select_fusion), calls=%async_computation | async-start | bytes 2097152 | tf_op jit(solution)/shard_map/all_to_all | solution.py:74
  29.5 0.8 fusion.18
  30.4 0.9 reduce-window.39
  31.7 22.5 %all-to-all-done = bf16[16,58,512]{2,1,0:T(8,128)(2,1)S(1)} async-done(((bf16[16,58,512]{2,1,0:T(8,128)(2,1)}), bf16[16,58,512]{2,1,0:T(8,128)(2,1)S(1)}, u32[]{:S(2)}, u32[]{:S(2)}) %all-to-all-start) | async-done | bytes 950304 | tf_op jit(solution)/shard_map/all_to_all | solution.py:74
  54.4 2.1 %gather_fusion.1 = bf16[384,512]{1,0:T(8,128)(2,1)S(1)} fusion(bf16[928,512]{1,0:T(8,128)(2,1)S(1)} %all_to_all.15, s32[1024]{0:T(1024)S(1)} %pad_clamp_fusion.1), kind=kCustom, calls=%fused_computation.1 | custom fusion | bytes 787968 | tf_op jit(solution)/shard_map/gather | solution.py:95
  57.0 38.6 %while.18 = (s32[]{:T(128)}, bf16[384,512]{1,0:T(8,128)(2,1)S(1)}, bf16[384,512]{1,0:T(8,128)(2,1)S(1)}, f32[384]{0:T(512)S(1)}, s32[384]{0:T(512)S(1)}, /*index...) while((s32[]{:T(128)}, bf16[384,512]{1,0:T(8,128)(2,1)S(1)}, ...), condition=%wide.region_26.27_spmd.clone, body=%wide.region_21.26_spmd.clone.sunk | while | flops 303321984 | bytes 6322649 | solution.py:116
  57.0 2.9 %collective-permute-start = (bf16[384,512]{1,0:T(8,128)(2,1)S(1)}, bf16[384,512]{1,0:T(8,128)(2,1)S(1)}, u32[]{:S(2)}, u32[]{:S(2)}) collective-permute-start(bf16[384,512]{1,0:T(8,128)(2,1)S(1)} %get-tuple-element.275), channel_id=1, source_target_pairs={{0,1},{1,2},{2,3},{3,4},{4,5},{5,6},{6,7},{7,8},{8,9},{9,10},{10,1... | collective-permute-start | bytes 1179656 | tf_op jit(solution)/shard_map/while/body/eval_jaxpr/ppermute | solution.py:13
  59.9 3.5 %collective-permute-start.1 = (bf16[384,512]{1,0:T(8,128)(2,1)S(1)}, bf16[384,512]{1,0:T(8,128)(2,1)S(1)}, u32[]{:S(2)}, u32[]{:S(2)}) collective-permute-start(bf16[384,512]{1,0:T(8,128)(2,1)S(1)} %get-tuple-element.276), channel_id=1, source_target_pairs={{1,0},{2,1},{3,2},{4,3},{5,4},{6,5},{7,6},{8,7},{9,8},{10,9},{11,1... | collective-permute-start | bytes 1179656 | tf_op jit(solution)/shard_map/while/body/eval_jaxpr/ppermute | solution.py:13
  63.6 5.1 %collective-permute-done.1 = bf16[384,512]{1,0:T(8,128)(2,1)S(1)} collective-permute-done((bf16[384,512]{1,0:T(8,128)(2,1)S(1)}, bf16[384,512]{1,0:T(8,128)(2,1)S(1)}, u32[]{:S(2)}, u32[]{:S(2)}) %collective-permute-start.1) | collective-permute-done | bytes 393248 | tf_op jit(solution)/shard_map/while/body/eval_jaxpr/ppermute | solution.py:13
  69.7 4.3 %collective-permute-start = (bf16[384,512]{1,0:T(8,128)(2,1)S(1)}, bf16[384,512]{1,0:T(8,128)(2,1)S(1)}, u32[]{:S(2)}, u32[]{:S(2)}) collective-permute-start(bf16[384,512]{1,0:T(8,128)(2,1)S(1)} %get-tuple-element.275), channel_id=1, source_target_pairs={{0,1},{1,2},{2,3},{3,4},{4,5},{5,6},{6,7},{7,8},{8,9},{9,10},{10,1... | collective-permute-start | bytes 1179656 | tf_op jit(solution)/shard_map/while/body/eval_jaxpr/ppermute | solution.py:13
  74.0 2.3 %collective-permute-start.1 = (bf16[384,512]{1,0:T(8,128)(2,1)S(1)}, bf16[384,512]{1,0:T(8,128)(2,1)S(1)}, u32[]{:S(2)}, u32[]{:S(2)}) collective-permute-start(bf16[384,512]{1,0:T(8,128)(2,1)S(1)} %get-tuple-element.276), channel_id=1, source_target_pairs={{1,0},{2,1},{3,2},{4,3},{5,4},{6,5},{7,6},{8,7},{9,8},{10,9},{11,1... | collective-permute-start | bytes 1179656 | tf_op jit(solution)/shard_map/while/body/eval_jaxpr/ppermute | solution.py:13
  76.5 5.2 %collective-permute-done.1 = bf16[384,512]{1,0:T(8,128)(2,1)S(1)} collective-permute-done((bf16[384,512]{1,0:T(8,128)(2,1)S(1)}, bf16[384,512]{1,0:T(8,128)(2,1)S(1)}, u32[]{:S(2)}, u32[]{:S(2)}) %collective-permute-start.1) | collective-permute-done | bytes 393248 | tf_op jit(solution)/shard_map/while/body/eval_jaxpr/ppermute | solution.py:13
  82.6 4.2 %collective-permute-start = (bf16[384,512]{1,0:T(8,128)(2,1)S(1)}, bf16[384,512]{1,0:T(8,128)(2,1)S(1)}, u32[]{:S(2)}, u32[]{:S(2)}) collective-permute-start(bf16[384,512]{1,0:T(8,128)(2,1)S(1)} %get-tuple-element.275), channel_id=1, source_target_pairs={{0,1},{1,2},{2,3},{3,4},{4,5},{5,6},{6,7},{7,8},{8,9},{9,10},{10,1... | collective-permute-start | bytes 1179656 | tf_op jit(solution)/shard_map/while/body/eval_jaxpr/ppermute | solution.py:13
  86.8 2.4 %collective-permute-start.1 = (bf16[384,512]{1,0:T(8,128)(2,1)S(1)}, bf16[384,512]{1,0:T(8,128)(2,1)S(1)}, u32[]{:S(2)}, u32[]{:S(2)}) collective-permute-start(bf16[384,512]{1,0:T(8,128)(2,1)S(1)} %get-tuple-element.276), channel_id=1, source_target_pairs={{1,0},{2,1},{3,2},{4,3},{5,4},{6,5},{7,6},{8,7},{9,8},{10,9},{11,1... | collective-permute-start | bytes 1179656 | tf_op jit(solution)/shard_map/while/body/eval_jaxpr/ppermute | solution.py:13
  89.4 5.2 %collective-permute-done.1 = bf16[384,512]{1,0:T(8,128)(2,1)S(1)} collective-permute-done((bf16[384,512]{1,0:T(8,128)(2,1)S(1)}, bf16[384,512]{1,0:T(8,128)(2,1)S(1)}, u32[]{:S(2)}, u32[]{:S(2)}) %collective-permute-start.1) | collective-permute-done | bytes 393248 | tf_op jit(solution)/shard_map/while/body/eval_jaxpr/ppermute | solution.py:13
  95.5 2.9 %scatter_custom_fusion.2 = f32[928]{0:T(1024)S(1)} fusion(s32[384]{0:T(512)S(1)} %fusion.57, f32[384]{0:T(512)S(1)} %get-tuple-element.141, f32[]{:T(128)} %constant.139.clone.1), kind=kCustom, calls=%fused_computation.128 | custom fusion | bytes 3716 | tf_op jit(solution)/shard_map/scatter | solution.py:119
  98.5 0.7 all_to_all.16
  99.1 8.8 %all-to-all-start.1 = ((f32[16,58,1]{1,2,0:T(1,128)}), f32[16,58,1]{1,2,0:T(1,128)S(1)}, u32[]{:S(2)}, u32[]{:S(2)}) async-start(f32[16,58,1]{1,2,0:T(1,128)} %bitcast.9), calls=%async_computation.1 | async-start | bytes 16384 | tf_op jit(solution)/shard_map/all_to_all | solution.py:121
  107.9 22.5 %all-reduce.2.cloned.1.call-done = f32[64,512]{1,0:T(8,128)} async-done(((f32[64,512]{1,0:T(8,128)}), f32[64,512]{1,0:T(8,128)}) %all-reduce.2.cloned.1.call-update) | async-done | bytes 131088 | tf_op jit(solution)/shard_map/psum | solution.py:132
  130.4 1.4 fusion.13
  131.8 0.5 broadcast.549
  132.3 0.7 reduce.13
  133.0 1.9 %gather_fusion.2 = f32[384]{0:T(512)S(1)} fusion(f32[928]{0:T(1024)S(1)} %all_to_all.18, s32[1024]{0:T(1024)S(1)} %pad_clamp_fusion), kind=kCustom, calls=%fused_computation.2 | custom fusion | bytes 4608 | tf_op jit(solution)/shard_map/gather | solution.py:122
  134.9 0.6 convert_divide_fusion
  (78 shorter events, 6.6 us)
Async XLA Ops:
  7.2 1.2 copy-start
  8.6 0.7 copy-start.2
  9.9 0.7 copy-start.1
  23.1 31.0 %all-to-all-start = ((bf16[16,58,512]{2,1,0:T(8,128)(2,1)}), bf16[16,58,512]{2,1,0:T(8,128)(2,1)S(1)}, u32[]{:S(2)}, u32[]{:S(2)}) async-start(bf16[16,58,512]{2,1,0:T(8,128)(2,1)} %broadcast_select_fusion), calls=%async_computation | async-start | bytes 2097152 | tf_op jit(solution)/shard_map/all_to_all | solution.py:74
  29.4 101.0 %all-reduce.2.cloned.1.call-start = ((), (), s32[]{:S(2)}) async-start(), calls=%async_computation.2 | async-start | bytes 262144 | tf_op jit(solution)/shard_map/psum | solution.py:132
  57.0 12.2 %collective-permute-start = (bf16[384,512]{1,0:T(8,128)(2,1)S(1)}, bf16[384,512]{1,0:T(8,128)(2,1)S(1)}, u32[]{:S(2)}, u32[]{:S(2)}) collective-permute-start(bf16[384,512]{1,0:T(8,128)(2,1)S(1)} %get-tuple-element.275), channel_id=1, source_target_pairs={{0,1},{1,2},{2,3},{3,4},{4,5},{5,6},{6,7},{7,8},{8,9},{9,10},{10,1... | collective-permute-start | bytes 1179656 | tf_op jit(solution)/shard_map/while/body/eval_jaxpr/ppermute | solution.py:13
  59.9 8.8 %collective-permute-start.1 = (bf16[384,512]{1,0:T(8,128)(2,1)S(1)}, bf16[384,512]{1,0:T(8,128)(2,1)S(1)}, u32[]{:S(2)}, u32[]{:S(2)}) collective-permute-start(bf16[384,512]{1,0:T(8,128)(2,1)S(1)} %get-tuple-element.276), channel_id=1, source_target_pairs={{1,0},{2,1},{3,2},{4,3},{5,4},{6,5},{7,6},{8,7},{9,8},{10,9},{11,1... | collective-permute-start | bytes 1179656 | tf_op jit(solution)/shard_map/while/body/eval_jaxpr/ppermute | solution.py:13
  69.7 12.4 %collective-permute-start = (bf16[384,512]{1,0:T(8,128)(2,1)S(1)}, bf16[384,512]{1,0:T(8,128)(2,1)S(1)}, u32[]{:S(2)}, u32[]{:S(2)}) collective-permute-start(bf16[384,512]{1,0:T(8,128)(2,1)S(1)} %get-tuple-element.275), channel_id=1, source_target_pairs={{0,1},{1,2},{2,3},{3,4},{4,5},{5,6},{6,7},{7,8},{8,9},{9,10},{10,1... | collective-permute-start | bytes 1179656 | tf_op jit(solution)/shard_map/while/body/eval_jaxpr/ppermute | solution.py:13
  74.0 7.7 %collective-permute-start.1 = (bf16[384,512]{1,0:T(8,128)(2,1)S(1)}, bf16[384,512]{1,0:T(8,128)(2,1)S(1)}, u32[]{:S(2)}, u32[]{:S(2)}) collective-permute-start(bf16[384,512]{1,0:T(8,128)(2,1)S(1)} %get-tuple-element.276), channel_id=1, source_target_pairs={{1,0},{2,1},{3,2},{4,3},{5,4},{6,5},{7,6},{8,7},{9,8},{10,9},{11,1... | collective-permute-start | bytes 1179656 | tf_op jit(solution)/shard_map/while/body/eval_jaxpr/ppermute | solution.py:13
  82.6 12.4 %collective-permute-start = (bf16[384,512]{1,0:T(8,128)(2,1)S(1)}, bf16[384,512]{1,0:T(8,128)(2,1)S(1)}, u32[]{:S(2)}, u32[]{:S(2)}) collective-permute-start(bf16[384,512]{1,0:T(8,128)(2,1)S(1)} %get-tuple-element.275), channel_id=1, source_target_pairs={{0,1},{1,2},{2,3},{3,4},{4,5},{5,6},{6,7},{7,8},{8,9},{9,10},{10,1... | collective-permute-start | bytes 1179656 | tf_op jit(solution)/shard_map/while/body/eval_jaxpr/ppermute | solution.py:13
  86.8 7.7 %collective-permute-start.1 = (bf16[384,512]{1,0:T(8,128)(2,1)S(1)}, bf16[384,512]{1,0:T(8,128)(2,1)S(1)}, u32[]{:S(2)}, u32[]{:S(2)}) collective-permute-start(bf16[384,512]{1,0:T(8,128)(2,1)S(1)} %get-tuple-element.276), channel_id=1, source_target_pairs={{1,0},{2,1},{3,2},{4,3},{5,4},{6,5},{7,6},{8,7},{9,8},{10,9},{11,1... | collective-permute-start | bytes 1179656 | tf_op jit(solution)/shard_map/while/body/eval_jaxpr/ppermute | solution.py:13
  99.1 32.6 %all-to-all-start.1 = ((f32[16,58,1]{1,2,0:T(1,128)}), f32[16,58,1]{1,2,0:T(1,128)S(1)}, u32[]{:S(2)}, u32[]{:S(2)}) async-start(f32[16,58,1]{1,2,0:T(1,128)} %bitcast.9), calls=%async_computation.1 | async-start | bytes 16384 | tf_op jit(solution)/shard_map/all_to_all | solution.py:121
Sparse Core Ops, SparseCore 0:
  33.7 96.6 all-reduce.1
where the time goes:
time: 143 us; the launch traced here: 142 us
  waiting for transfers between devices  60.5 us (42%)
  starting transfers between devices  34.8 us (24%)
  local copies, waits for them, and re-layouts  19.8 us (14%)
  between operations  14.3 us (10%)
  other arithmetic  7.29 us (5%)
  matrix products  5.41 us (4%)
    all_to_all x1, waiting for transfers between devices, sorted_density(): lax.all_to_all(packed, 'blk', split_axis=0, concat_axis=0, tiled=True)  22.5 us
    psum x1, waiting for transfers between devices, on_device(): centroid = lax.psum(partial_sum, 'blk')  22.5 us
    ppermute x6, starting transfers between devices, shifted(): return lax.ppermute(array, axis, pairs)  19.7 us
    ppermute x6, waiting for transfers between devices, shifted(): return lax.ppermute(array, axis, pairs)  15.5 us
    all_to_all x1, starting transfers between devices, sorted_density(): lax.all_to_all(returned, 'blk', split_axis=0, concat_axis=0, tiled=True)  8.78 us
    all_to_all x1, starting transfers between devices, sorted_density(): lax.all_to_all(packed, 'blk', split_axis=0, concat_axis=0, tiled=True)  6.3 us
    gather x2, local copies, waits for them, and re-layouts, sorted_density(): unit[sender]  4.29 us
    scatter x1, local copies, waits for them, and re-layouts, sorted_density(): sender = jnp.zeros((devices * capacity,), jnp.int32).at[address].set(jnp....  2.92 us
  transfers between devices with their start and end apart: 9, of which 5 were waited for; matrix products, arithmetic and copies ran while one was open for 8% of the time, Pallas kernels for 0%

commit v1 on v0

--- a/solution.py
+++ b/solution.py
@@ -5,6 +5,29 @@
 
 SOFTMAX_TEMP = 0.1
 EPSILON = 1e-06
+
+
+def in_blocks(shard, dim, size):
+    shape = shard.shape
+    parts = shard.reshape(*shape[:dim], size, shape[dim] // size, *shape[dim + 1 :])
+    return jnp.moveaxis(parts, dim, 0)
+
+
+def joined_along(blocks, dim):
+    blocks = jnp.moveaxis(blocks, 0, dim)
+    shape = blocks.shape
+    return blocks.reshape(*shape[:dim], shape[dim] * shape[dim + 1], *shape[dim + 2 :])
+
+
+def sent_to_each(array, axis, split_dim, concat_dim):
+    peers, index = (lax.axis_size(axis), lax.axis_index(axis))
+    tiles = in_blocks(array, split_dim, peers)
+    finished = [tiles[index]]
+    for step in range(1, peers):
+        sent = tiles[(index + step) % peers]
+        finished.append(lax.ppermute(sent, axis, [(i, (i + step) % peers) for i in range(peers)]))
+    tiles = jnp.stack(finished)[(index - jnp.arange(peers)) % peers]
+    return joined_along(tiles, concat_dim)
 
 
 def shifted(array, axis, by):
@@ -71,7 +94,7 @@
     )
     filled = jnp.zeros((devices * capacity,), jnp.bool_).at[address].set(True)
     packed = jnp.where(filled[:, None], unit[sender], jnp.zeros((), jnp.bfloat16))
-    arrived = lax.all_to_all(packed, "blk", split_axis=0, concat_axis=0, tiled=True)
+    arrived = sent_to_each(packed, "blk", 0, 0)
     local = jnp.arange(rows_dev, dtype=jnp.int32)
     places = own_index * rows_dev + local
     home_label = jnp.sum((places[:, None] >= ends[None, :]).astype(jnp.int32), axis=1)

time: 143 us -> 127 us (0.89)
  the two profiles are of different devices: /device:TPU:8 before, /device:TPU:0 now
where the time goes in v1:
time: 127 us; the launch traced here: 126 us
  starting transfers between devices  55.5 us (44%)
  waiting for transfers between devices  23.6 us (19%)
  local copies, waits for them, and re-layouts  20.6 us (16%)
  between operations  14.7 us (12%)
  other arithmetic  6.31 us (5%)
  matrix products  5.41 us (4%)
    ppermute x6, starting transfers between devices, shifted(): return lax.ppermute(array, axis, pairs)  23.7 us
    ppermute x15, starting transfers between devices, sent_to_each(): lax.ppermute(sent, axis, [(i, (i + step) % peers) for i in range(peers)])  22.2 us
    all_to_all x1, starting transfers between devices, sorted_density(): lax.all_to_all(returned, 'blk', split_axis=0, concat_axis=0, tiled=True)  9.63 us
    ppermute x15, waiting for transfers between devices, sent_to_each(): lax.ppermute(sent, axis, [(i, (i + step) % peers) for i in range(peers)])  9.49 us
    ppermute x6, waiting for transfers between devices, shifted(): return lax.ppermute(array, axis, pairs)  9.08 us
    all_to_all x1, waiting for transfers between devices, sorted_density(): lax.all_to_all(returned, 'blk', split_axis=0, concat_axis=0, tiled=True)  5.02 us
    gather x2, local copies, waits for them, and re-layouts, sorted_density(): unit[sender]  4.29 us
    scatter x1, local copies, waits for them, and re-layouts, sorted_density(): sender = jnp.zeros((devices * capacity,), jnp.int32).at[address].set(jnp....  2.92 us
  transfers between devices with their start and end apart: 23, of which 9 were waited for; matrix products, arithmetic and copies ran while one was open for 19% of the time, Pallas kernels for 0%

profile of v1, /device:TPU:0, one launch (start us, length us, event | category | flops | bytes accessed | tf_op | source)
XLA Modules:
  0.0 126.4 jit_solution(6832929182432511807)
XLA Ops:
  7.2 1.2 fusion.14
  11.4 0.9 reduce-window.41
  13.0 0.9 reduce-window.39
  14.8 2.9 %scatter_custom_fusion.1 = s32[928]{0:T(1024)S(1)} fusion(s32[384]{0:T(512)S(1)} %fusion.59, s32[384]{0:T(512)S(1)} %iota.61, s32[]{:T(128)} %copy.55), kind=kCustom, calls=%fused_computation.157 | custom fusion | bytes 3716 | tf_op jit(solution)/shard_map/scatter | solution.py:93
  17.9 4.0 %gather_fusion = bf16[928,512]{1,0:T(8,128)(2,1)S(1)} fusion(bf16[384,512]{1,0:T(8,128)(2,1)S(1)} %fusion.15, s32[1024]{0:T(1024)S(1)} %get-tuple-element.222), kind=kCustom, calls=%fused_computation | custom fusion | bytes 1904256 | tf_op jit(solution)/shard_map/gather | solution.py:96
  22.2 2.0 %scatter_custom_fusion = pred[928]{0:T(1024)(128)(4,1)S(1)} fusion(s32[384]{0:T(512)S(1)} %fusion.59, pred[384]{0:T(512)(128)(4,1)S(1)} %broadcast.549, pred[]{:T(512)} %constant.238.clone.1), kind=kCustom, calls=%fused_computation.170 | custom fusion | bytes 929 | tf_op jit(solution)/shard_map/scatter | solution.py:95
  25.3 2.6 %collective-permute-start.3 = (bf16[58,512]{1,0:T(8,128)(2,1)S(1)}, bf16[58,512]{1,0:T(8,128)(2,1)S(1)}, u32[]{:S(2)}, u32[]{:S(2)}) collective-permute-start(bf16[58,512]{1,0:T(8,128)(2,1)S(1)} %get-tuple-element.207), channel_id=1, source_target_pairs={{0,2},{1,3},{2,4},{3,5},{4,6},{5,7},{6,8},{7,9},{8,10},{9,11},{10,... | collective-permute-start | bytes 178184 | tf_op jit(solution)/shard_map/ppermute | solution.py:28
  27.9 2.4 %collective-permute-start.4 = (bf16[58,512]{1,0:T(8,128)(2,1)S(1)}, bf16[58,512]{1,0:T(8,128)(2,1)S(1)}, u32[]{:S(2)}, u32[]{:S(2)}) collective-permute-start(bf16[58,512]{1,0:T(8,128)(2,1)S(1)} %get-tuple-element.206), channel_id=1, source_target_pairs={{0,3},{1,4},{2,5},{3,6},{4,7},{5,8},{6,9},{7,10},{8,11},{9,12},{10... | collective-permute-start | bytes 178184 | tf_op jit(solution)/shard_map/ppermute | solution.py:28
  30.3 1.6 %collective-permute-start.5 = (bf16[58,512]{1,0:T(8,128)(2,1)S(1)}, bf16[58,512]{1,0:T(8,128)(2,1)S(1)}, u32[]{:S(2)}, u32[]{:S(2)}) collective-permute-start(bf16[58,512]{1,0:T(8,128)(2,1)S(1)} %get-tuple-element.205), channel_id=1, source_target_pairs={{0,4},{1,5},{2,6},{3,7},{4,8},{5,9},{6,10},{7,11},{8,12},{9,13},{1... | collective-permute-start | bytes 178184 | tf_op jit(solution)/shard_map/ppermute | solution.py:28
  32.3 1.0 collective-permute-start.7
  33.4 4.4 %collective-permute-start.8 = (bf16[58,512]{1,0:T(8,128)(2,1)S(1)}, bf16[58,512]{1,0:T(8,128)(2,1)S(1)}, u32[]{:S(2)}, u32[]{:S(2)}) collective-permute-start(bf16[58,512]{1,0:T(8,128)(2,1)S(1)} %get-tuple-element.202), channel_id=1, source_target_pairs={{0,7},{1,8},{2,9},{3,10},{4,11},{5,12},{6,13},{7,14},{8,15},{9,0},... | collective-permute-start | bytes 178184 | tf_op jit(solution)/shard_map/ppermute | solution.py:28
  38.5 6.6 %collective-permute-done.6 = bf16[58,512]{1,0:T(8,128)(2,1)S(1)} collective-permute-done((bf16[58,512]{1,0:T(8,128)(2,1)S(1)}, bf16[58,512]{1,0:T(8,128)(2,1)S(1)}, u32[]{:S(2)}, u32[]{:S(2)}) %collective-permute-start.6) | collective-permute-done | bytes 59424 | tf_op jit(solution)/shard_map/ppermute | solution.py:28
  45.9 3.9 %collective-permute-start.13 = (bf16[58,512]{1,0:T(8,128)(2,1)S(1)}, bf16[58,512]{1,0:T(8,128)(2,1)S(1)}, u32[]{:S(2)}, u32[]{:S(2)}) collective-permute-start(bf16[58,512]{1,0:T(8,128)(2,1)S(1)} %get-tuple-element.197), channel_id=1, source_target_pairs={{0,12},{1,13},{2,14},{3,15},{4,0},{5,1},{6,2},{7,3},{8,4},{9,5},{1... | collective-permute-start | bytes 178184 | tf_op jit(solution)/shard_map/ppermute | solution.py:28
  50.6 2.7 %collective-permute-start.15 = (bf16[58,512]{1,0:T(8,128)(2,1)S(1)}, bf16[58,512]{1,0:T(8,128)(2,1)S(1)}, u32[]{:S(2)}, u32[]{:S(2)}) collective-permute-start(bf16[58,512]{1,0:T(8,128)(2,1)S(1)} %get-tuple-element.195), channel_id=1, source_target_pairs={{0,14},{1,15},{2,0},{3,1},{4,2},{5,3},{6,4},{7,5},{8,6},{9,7},{10,... | collective-permute-start | bytes 178184 | tf_op jit(solution)/shard_map/ppermute | solution.py:28
  53.3 0.9 collective-permute-start.16
  54.2 1.5 %collective-permute-done.15 = bf16[58,512]{1,0:T(8,128)(2,1)S(1)} collective-permute-done((bf16[58,512]{1,0:T(8,128)(2,1)S(1)}, bf16[58,512]{1,0:T(8,128)(2,1)S(1)}, u32[]{:S(2)}, u32[]{:S(2)}) %collective-permute-start.15) | collective-permute-done | bytes 59424 | tf_op jit(solution)/shard_map/ppermute | solution.py:28
  57.5 2.1 %gather_fusion.2 = bf16[384,512]{1,0:T(8,128)(2,1)S(1)} fusion(bf16[928,512]{1,0:T(8,128)(2,1)S(1)} %reshape.459, s32[1024]{0:T(1024)S(1)} %get-tuple-element.221), kind=kCustom, calls=%fused_computation.2 | custom fusion | bytes 787968 | tf_op jit(solution)/shard_map/gather | solution.py:118
  60.1 36.0 %while.18 = (s32[]{:T(128)}, bf16[384,512]{1,0:T(8,128)(2,1)S(1)}, bf16[384,512]{1,0:T(8,128)(2,1)S(1)}, f32[384]{0:T(512)S(1)}, s32[384]{0:T(512)S(1)}, /*index...) while((s32[]{:T(128)}, bf16[384,512]{1,0:T(8,128)(2,1)S(1)}, ...), condition=%wide.region_26.27_spmd.clone, body=%wide.region_21.26_spmd.clone.sunk | while | flops 303321984 | bytes 6322649 | solution.py:139
  60.1 3.4 %collective-permute-start = (bf16[384,512]{1,0:T(8,128)(2,1)S(1)}, bf16[384,512]{1,0:T(8,128)(2,1)S(1)}, u32[]{:S(2)}, u32[]{:S(2)}) collective-permute-start(bf16[384,512]{1,0:T(8,128)(2,1)S(1)} %get-tuple-element.291), channel_id=1, source_target_pairs={{0,1},{1,2},{2,3},{3,4},{4,5},{5,6},{6,7},{7,8},{8,9},{9,10},{10,1... | collective-permute-start | bytes 1179656 | tf_op jit(solution)/shard_map/while/body/eval_jaxpr/ppermute | solution.py:36
  63.5 1.3 %collective-permute-start.1 = (bf16[384,512]{1,0:T(8,128)(2,1)S(1)}, bf16[384,512]{1,0:T(8,128)(2,1)S(1)}, u32[]{:S(2)}, u32[]{:S(2)}) collective-permute-start(bf16[384,512]{1,0:T(8,128)(2,1)S(1)} %get-tuple-element.292), channel_id=1, source_target_pairs={{1,0},{2,1},{3,2},{4,3},{5,4},{6,5},{7,6},{8,7},{9,8},{10,9},{11,1... | collective-permute-start | bytes 1179656 | tf_op jit(solution)/shard_map/while/body/eval_jaxpr/ppermute | solution.py:36
  65.0 2.4 %collective-permute-done.1 = bf16[384,512]{1,0:T(8,128)(2,1)S(1)} collective-permute-done((bf16[384,512]{1,0:T(8,128)(2,1)S(1)}, bf16[384,512]{1,0:T(8,128)(2,1)S(1)}, u32[]{:S(2)}, u32[]{:S(2)}) %collective-permute-start.1) | collective-permute-done | bytes 393248 | tf_op jit(solution)/shard_map/while/body/eval_jaxpr/ppermute | solution.py:36
  68.3 8.5 %collective-permute-start = (bf16[384,512]{1,0:T(8,128)(2,1)S(1)}, bf16[384,512]{1,0:T(8,128)(2,1)S(1)}, u32[]{:S(2)}, u32[]{:S(2)}) collective-permute-start(bf16[384,512]{1,0:T(8,128)(2,1)S(1)} %get-tuple-element.291), channel_id=1, source_target_pairs={{0,1},{1,2},{2,3},{3,4},{4,5},{5,6},{6,7},{7,8},{8,9},{9,10},{10,1... | collective-permute-start | bytes 1179656 | tf_op jit(solution)/shard_map/while/body/eval_jaxpr/ppermute | solution.py:36
  76.8 1.3 %collective-permute-start.1 = (bf16[384,512]{1,0:T(8,128)(2,1)S(1)}, bf16[384,512]{1,0:T(8,128)(2,1)S(1)}, u32[]{:S(2)}, u32[]{:S(2)}) collective-permute-start(bf16[384,512]{1,0:T(8,128)(2,1)S(1)} %get-tuple-element.292), channel_id=1, source_target_pairs={{1,0},{2,1},{3,2},{4,3},{5,4},{6,5},{7,6},{8,7},{9,8},{10,9},{11,1... | collective-permute-start | bytes 1179656 | tf_op jit(solution)/shard_map/while/body/eval_jaxpr/ppermute | solution.py:36
  78.2 3.1 %collective-permute-done.1 = bf16[384,512]{1,0:T(8,128)(2,1)S(1)} collective-permute-done((bf16[384,512]{1,0:T(8,128)(2,1)S(1)}, bf16[384,512]{1,0:T(8,128)(2,1)S(1)}, u32[]{:S(2)}, u32[]{:S(2)}) %collective-permute-start.1) | collective-permute-done | bytes 393248 | tf_op jit(solution)/shard_map/while/body/eval_jaxpr/ppermute | solution.py:36
  82.3 7.9 %collective-permute-start = (bf16[384,512]{1,0:T(8,128)(2,1)S(1)}, bf16[384,512]{1,0:T(8,128)(2,1)S(1)}, u32[]{:S(2)}, u32[]{:S(2)}) collective-permute-start(bf16[384,512]{1,0:T(8,128)(2,1)S(1)} %get-tuple-element.291), channel_id=1, source_target_pairs={{0,1},{1,2},{2,3},{3,4},{4,5},{5,6},{6,7},{7,8},{8,9},{9,10},{10,1... | collective-permute-start | bytes 1179656 | tf_op jit(solution)/shard_map/while/body/eval_jaxpr/ppermute | solution.py:36
  90.2 1.3 %collective-permute-start.1 = (bf16[384,512]{1,0:T(8,128)(2,1)S(1)}, bf16[384,512]{1,0:T(8,128)(2,1)S(1)}, u32[]{:S(2)}, u32[]{:S(2)}) collective-permute-start(bf16[384,512]{1,0:T(8,128)(2,1)S(1)} %get-tuple-element.292), channel_id=1, source_target_pairs={{1,0},{2,1},{3,2},{4,3},{5,4},{6,5},{7,6},{8,7},{9,8},{10,9},{11,1... | collective-permute-start | bytes 1179656 | tf_op jit(solution)/shard_map/while/body/eval_jaxpr/ppermute | solution.py:36
  91.6 3.5 %collective-permute-done.1 = bf16[384,512]{1,0:T(8,128)(2,1)S(1)} collective-permute-done((bf16[384,512]{1,0:T(8,128)(2,1)S(1)}, bf16[384,512]{1,0:T(8,128)(2,1)S(1)}, u32[]{:S(2)}, u32[]{:S(2)}) %collective-permute-start.1) | collective-permute-done | bytes 393248 | tf_op jit(solution)/shard_map/while/body/eval_jaxpr/ppermute | solution.py:36
  96.1 2.9 %scatter_custom_fusion.2 = f32[928]{0:T(1024)S(1)} fusion(s32[384]{0:T(512)S(1)} %fusion.58, f32[384]{0:T(512)S(1)} %get-tuple-element.141, f32[]{:T(128)} %constant.225.clone.1), kind=kCustom, calls=%fused_computation.165 | custom fusion | bytes 3716 | tf_op jit(solution)/shard_map/scatter | solution.py:142
  99.7 9.6 %all-to-all-start = ((f32[16,58,1]{1,2,0:T(1,128)}), f32[16,58,1]{1,2,0:T(1,128)S(1)}, u32[]{:S(2)}, u32[]{:S(2)}) async-start(f32[16,58,1]{1,2,0:T(1,128)} %bitcast.40), calls=%async_computation | async-start | bytes 16384 | tf_op jit(solution)/shard_map/all_to_all | solution.py:144
  109.4 1.4 %fusion.13 = f32[384]{0:T(512)S(1)} fusion(bf16[384,512]{1,0:T(8,128)(2,1)S(1)} %fusion.15, f32[64,512]{1,0:T(8,128)} %all-reduce.2.cloned.1.call-done, s32[384]{0:T(512)S(1)} %copy-done.1), kind=kOutput, calls=%fused_computation.29 | convolution fusion | flops 151068288 | bytes 527360 | tf_op jit(solution)/shard_map/dot_general | solution.py:159
  110.8 5.0 %all-to-all-done = f32[16,58,1]{1,2,0:T(1,128)S(1)} async-done(((f32[16,58,1]{1,2,0:T(1,128)}), f32[16,58,1]{1,2,0:T(1,128)S(1)}, u32[]{:S(2)}, u32[]{:S(2)}) %all-to-all-start) | async-done | bytes 3744 | tf_op jit(solution)/shard_map/all_to_all | solution.py:144
  117.1 1.9 %gather_fusion.3 = f32[384]{0:T(512)S(1)} fusion(f32[928]{0:T(1024)S(1)} %all_to_all.10, s32[1024]{0:T(1024)S(1)} %pad_clamp_fusion), kind=kCustom, calls=%fused_computation.3 | custom fusion | bytes 4608 | tf_op jit(solution)/shard_map/gather | solution.py:145
  (125 shorter events, 16.3 us)
Async XLA Ops:
  7.2 1.3 copy-start
  7.2 102.2 %all-reduce.2.cloned.1.call-start = ((), (), s32[]{:S(2)}) async-start(), calls=%async_computation.1 | async-start | bytes 262144 | tf_op jit(solution)/shard_map/psum | solution.py:155
  8.4 0.7 copy-start.1
  10.0 0.7 copy-start.2
  24.8 7.6 %collective-permute-start.2 = (bf16[58,512]{1,0:T(8,128)(2,1)S(1)}, bf16[58,512]{1,0:T(8,128)(2,1)S(1)}, u32[]{:S(2)}, u32[]{:S(2)}) collective-permute-start(bf16[58,512]{1,0:T(8,128)(2,1)S(1)} %get-tuple-element.208), channel_id=1, source_target_pairs={{0,1},{1,2},{2,3},{3,4},{4,5},{5,6},{6,7},{7,8},{8,9},{9,10},{10,1... | collective-permute-start | bytes 178184 | tf_op jit(solution)/shard_map/ppermute | solution.py:28
  25.3 8.1 %collective-permute-start.3 = (bf16[58,512]{1,0:T(8,128)(2,1)S(1)}, bf16[58,512]{1,0:T(8,128)(2,1)S(1)}, u32[]{:S(2)}, u32[]{:S(2)}) collective-permute-start(bf16[58,512]{1,0:T(8,128)(2,1)S(1)} %get-tuple-element.207), channel_id=1, source_target_pairs={{0,2},{1,3},{2,4},{3,5},{4,6},{5,7},{6,8},{7,9},{8,10},{9,11},{10,... | collective-permute-start | bytes 178184 | tf_op jit(solution)/shard_map/ppermute | solution.py:28
  27.9 9.9 %collective-permute-start.4 = (bf16[58,512]{1,0:T(8,128)(2,1)S(1)}, bf16[58,512]{1,0:T(8,128)(2,1)S(1)}, u32[]{:S(2)}, u32[]{:S(2)}) collective-permute-start(bf16[58,512]{1,0:T(8,128)(2,1)S(1)} %get-tuple-element.206), channel_id=1, source_target_pairs={{0,3},{1,4},{2,5},{3,6},{4,7},{5,8},{6,9},{7,10},{8,11},{9,12},{10... | collective-permute-start | bytes 178184 | tf_op jit(solution)/shard_map/ppermute | solution.py:28
  30.3 7.9 %collective-permute-start.5 = (bf16[58,512]{1,0:T(8,128)(2,1)S(1)}, bf16[58,512]{1,0:T(8,128)(2,1)S(1)}, u32[]{:S(2)}, u32[]{:S(2)}) collective-permute-start(bf16[58,512]{1,0:T(8,128)(2,1)S(1)} %get-tuple-element.205), channel_id=1, source_target_pairs={{0,4},{1,5},{2,6},{3,7},{4,8},{5,9},{6,10},{7,11},{8,12},{9,13},{1... | collective-permute-start | bytes 178184 | tf_op jit(solution)/shard_map/ppermute | solution.py:28
  31.9 13.3 %collective-permute-start.6 = (bf16[58,512]{1,0:T(8,128)(2,1)S(1)}, bf16[58,512]{1,0:T(8,128)(2,1)S(1)}, u32[]{:S(2)}, u32[]{:S(2)}) collective-permute-start(bf16[58,512]{1,0:T(8,128)(2,1)S(1)} %get-tuple-element.204), channel_id=1, source_target_pairs={{0,5},{1,6},{2,7},{3,8},{4,9},{5,10},{6,11},{7,12},{8,13},{9,14},{... | collective-permute-start | bytes 178184 | tf_op jit(solution)/shard_map/ppermute | solution.py:28
  32.3 13.1 %collective-permute-start.7 = (bf16[58,512]{1,0:T(8,128)(2,1)S(1)}, bf16[58,512]{1,0:T(8,128)(2,1)S(1)}, u32[]{:S(2)}, u32[]{:S(2)}) collective-permute-start(bf16[58,512]{1,0:T(8,128)(2,1)S(1)} %get-tuple-element.203), channel_id=1, source_target_pairs={{0,6},{1,7},{2,8},{3,9},{4,10},{5,11},{6,12},{7,13},{8,14},{9,15},... | collective-permute-start | bytes 178184 | tf_op jit(solution)/shard_map/ppermute | solution.py:28
  33.4 12.5 %collective-permute-start.8 = (bf16[58,512]{1,0:T(8,128)(2,1)S(1)}, bf16[58,512]{1,0:T(8,128)(2,1)S(1)}, u32[]{:S(2)}, u32[]{:S(2)}) collective-permute-start(bf16[58,512]{1,0:T(8,128)(2,1)S(1)} %get-tuple-element.202), channel_id=1, source_target_pairs={{0,7},{1,8},{2,9},{3,10},{4,11},{5,12},{6,13},{7,14},{8,15},{9,0},... | collective-permute-start | bytes 178184 | tf_op jit(solution)/shard_map/ppermute | solution.py:28
  37.8 12.0 %collective-permute-start.9 = (bf16[58,512]{1,0:T(8,128)(2,1)S(1)}, bf16[58,512]{1,0:T(8,128)(2,1)S(1)}, u32[]{:S(2)}, u32[]{:S(2)}) collective-permute-start(bf16[58,512]{1,0:T(8,128)(2,1)S(1)} %get-tuple-element.201), channel_id=1, source_target_pairs={{0,8},{1,9},{2,10},{3,11},{4,12},{5,13},{6,14},{7,15},{8,0},{9,1},... | collective-permute-start | bytes 178184 | tf_op jit(solution)/shard_map/ppermute | solution.py:28
  38.2 12.4 %collective-permute-start.10 = (bf16[58,512]{1,0:T(8,128)(2,1)S(1)}, bf16[58,512]{1,0:T(8,128)(2,1)S(1)}, u32[]{:S(2)}, u32[]{:S(2)}) collective-permute-start(bf16[58,512]{1,0:T(8,128)(2,1)S(1)} %get-tuple-element.200), channel_id=1, source_target_pairs={{0,9},{1,10},{2,11},{3,12},{4,13},{5,14},{6,15},{7,0},{8,1},{9,2},... | collective-permute-start | bytes 178184 | tf_op jit(solution)/shard_map/ppermute | solution.py:28
  45.2 8.1 %collective-permute-start.11 = (bf16[58,512]{1,0:T(8,128)(2,1)S(1)}, bf16[58,512]{1,0:T(8,128)(2,1)S(1)}, u32[]{:S(2)}, u32[]{:S(2)}) collective-permute-start(bf16[58,512]{1,0:T(8,128)(2,1)S(1)} %get-tuple-element.199), channel_id=1, source_target_pairs={{0,10},{1,11},{2,12},{3,13},{4,14},{5,15},{6,0},{7,1},{8,2},{9,3},... | collective-permute-start | bytes 178184 | tf_op jit(solution)/shard_map/ppermute | solution.py:28
  45.4 8.8 %collective-permute-start.12 = (bf16[58,512]{1,0:T(8,128)(2,1)S(1)}, bf16[58,512]{1,0:T(8,128)(2,1)S(1)}, u32[]{:S(2)}, u32[]{:S(2)}) collective-permute-start(bf16[58,512]{1,0:T(8,128)(2,1)S(1)} %get-tuple-element.198), channel_id=1, source_target_pairs={{0,11},{1,12},{2,13},{3,14},{4,15},{5,0},{6,1},{7,2},{8,3},{9,4},{... | collective-permute-start | bytes 178184 | tf_op jit(solution)/shard_map/ppermute | solution.py:28
  45.9 8.3 %collective-permute-start.13 = (bf16[58,512]{1,0:T(8,128)(2,1)S(1)}, bf16[58,512]{1,0:T(8,128)(2,1)S(1)}, u32[]{:S(2)}, u32[]{:S(2)}) collective-permute-start(bf16[58,512]{1,0:T(8,128)(2,1)S(1)} %get-tuple-element.197), channel_id=1, source_target_pairs={{0,12},{1,13},{2,14},{3,15},{4,0},{5,1},{6,2},{7,3},{8,4},{9,5},{1... | collective-permute-start | bytes 178184 | tf_op jit(solution)/shard_map/ppermute | solution.py:28
  49.8 4.4 %collective-permute-start.14 = (bf16[58,512]{1,0:T(8,128)(2,1)S(1)}, bf16[58,512]{1,0:T(8,128)(2,1)S(1)}, u32[]{:S(2)}, u32[]{:S(2)}) collective-permute-start(bf16[58,512]{1,0:T(8,128)(2,1)S(1)} %get-tuple-element.196), channel_id=1, source_target_pairs={{0,13},{1,14},{2,15},{3,0},{4,1},{5,2},{6,3},{7,4},{8,5},{9,6},{10... | collective-permute-start | bytes 178184 | tf_op jit(solution)/shard_map/ppermute | solution.py:28
  50.6 5.2 %collective-permute-start.15 = (bf16[58,512]{1,0:T(8,128)(2,1)S(1)}, bf16[58,512]{1,0:T(8,128)(2,1)S(1)}, u32[]{:S(2)}, u32[]{:S(2)}) collective-permute-start(bf16[58,512]{1,0:T(8,128)(2,1)S(1)} %get-tuple-element.195), channel_id=1, source_target_pairs={{0,14},{1,15},{2,0},{3,1},{4,2},{5,3},{6,4},{7,5},{8,6},{9,7},{10,... | collective-permute-start | bytes 178184 | tf_op jit(solution)/shard_map/ppermute | solution.py:28
  53.3 3.4 %collective-permute-start.16 = (bf16[58,512]{1,0:T(8,128)(2,1)S(1)}, bf16[58,512]{1,0:T(8,128)(2,1)S(1)}, u32[]{:S(2)}, u32[]{:S(2)}) collective-permute-start(bf16[58,512]{1,0:T(8,128)(2,1)S(1)} %get-tuple-element.194), channel_id=1, source_target_pairs={{0,15},{1,0},{2,1},{3,2},{4,3},{5,4},{6,5},{7,6},{8,7},{9,8},{10,9... | collective-permute-start | bytes 178184 | tf_op jit(solution)/shard_map/ppermute | solution.py:28
  60.1 7.7 %collective-permute-start = (bf16[384,512]{1,0:T(8,128)(2,1)S(1)}, bf16[384,512]{1,0:T(8,128)(2,1)S(1)}, u32[]{:S(2)}, u32[]{:S(2)}) collective-permute-start(bf16[384,512]{1,0:T(8,128)(2,1)S(1)} %get-tuple-element.291), channel_id=1, source_target_pairs={{0,1},{1,2},{2,3},{3,4},{4,5},{5,6},{6,7},{7,8},{8,9},{9,10},{10,1... | collective-permute-start | bytes 1179656 | tf_op jit(solution)/shard_map/while/body/eval_jaxpr/ppermute | solution.py:36
  63.5 3.9 %collective-permute-start.1 = (bf16[384,512]{1,0:T(8,128)(2,1)S(1)}, bf16[384,512]{1,0:T(8,128)(2,1)S(1)}, u32[]{:S(2)}, u32[]{:S(2)}) collective-permute-start(bf16[384,512]{1,0:T(8,128)(2,1)S(1)} %get-tuple-element.292), channel_id=1, source_target_pairs={{1,0},{2,1},{3,2},{4,3},{5,4},{6,5},{7,6},{8,7},{9,8},{10,9},{11,1... | collective-permute-start | bytes 1179656 | tf_op jit(solution)/shard_map/while/body/eval_jaxpr/ppermute | solution.py:36
  68.3 13.5 %collective-permute-start = (bf16[384,512]{1,0:T(8,128)(2,1)S(1)}, bf16[384,512]{1,0:T(8,128)(2,1)S(1)}, u32[]{:S(2)}, u32[]{:S(2)}) collective-permute-start(bf16[384,512]{1,0:T(8,128)(2,1)S(1)} %get-tuple-element.291), channel_id=1, source_target_pairs={{0,1},{1,2},{2,3},{3,4},{4,5},{5,6},{6,7},{7,8},{8,9},{9,10},{10,1... | collective-permute-start | bytes 1179656 | tf_op jit(solution)/shard_map/while/body/eval_jaxpr/ppermute | solution.py:36
  76.8 4.6 %collective-permute-start.1 = (bf16[384,512]{1,0:T(8,128)(2,1)S(1)}, bf16[384,512]{1,0:T(8,128)(2,1)S(1)}, u32[]{:S(2)}, u32[]{:S(2)}) collective-permute-start(bf16[384,512]{1,0:T(8,128)(2,1)S(1)} %get-tuple-element.292), channel_id=1, source_target_pairs={{1,0},{2,1},{3,2},{4,3},{5,4},{6,5},{7,6},{8,7},{9,8},{10,9},{11,1... | collective-permute-start | bytes 1179656 | tf_op jit(solution)/shard_map/while/body/eval_jaxpr/ppermute | solution.py:36
  82.3 13.3 %collective-permute-start = (bf16[384,512]{1,0:T(8,128)(2,1)S(1)}, bf16[384,512]{1,0:T(8,128)(2,1)S(1)}, u32[]{:S(2)}, u32[]{:S(2)}) collective-permute-start(bf16[384,512]{1,0:T(8,128)(2,1)S(1)} %get-tuple-element.291), channel_id=1, source_target_pairs={{0,1},{1,2},{2,3},{3,4},{4,5},{5,6},{6,7},{7,8},{8,9},{9,10},{10,1... | collective-permute-start | bytes 1179656 | tf_op jit(solution)/shard_map/while/body/eval_jaxpr/ppermute | solution.py:36
  90.2 5.0 %collective-permute-start.1 = (bf16[384,512]{1,0:T(8,128)(2,1)S(1)}, bf16[384,512]{1,0:T(8,128)(2,1)S(1)}, u32[]{:S(2)}, u32[]{:S(2)}) collective-permute-start(bf16[384,512]{1,0:T(8,128)(2,1)S(1)} %get-tuple-element.292), channel_id=1, source_target_pairs={{1,0},{2,1},{3,2},{4,3},{5,4},{6,5},{7,6},{8,7},{9,8},{10,9},{11,1... | collective-permute-start | bytes 1179656 | tf_op jit(solution)/shard_map/while/body/eval_jaxpr/ppermute | solution.py:36
  99.7 16.1 %all-to-all-start = ((f32[16,58,1]{1,2,0:T(1,128)}), f32[16,58,1]{1,2,0:T(1,128)S(1)}, u32[]{:S(2)}, u32[]{:S(2)}) async-start(f32[16,58,1]{1,2,0:T(1,128)} %bitcast.40), calls=%async_computation | async-start | bytes 16384 | tf_op jit(solution)/shard_map/all_to_all | solution.py:144
Sparse Core Ops, SparseCore 0:
  11.4 95.9 all-reduce.1
